TPU v7x, 128 devices: a whole 4x4x4 slice. The times are simulated.
128 devices in a mesh: teach: 2 (over core), dp: 64 (over x, z, y).
Axes of the slice: x: 4, y: 4, z: 4, core: 2. Of those that a mesh axis runs over, the one named last changes fastest.
Arguments:
- teacher_logits: bfloat16 [2, 16384, 5000], P('teach', 'dp'), may hold values from -18 to 400
- routes: int32 [16384, 1], P('dp'), may hold values from 0 to 127; in each aligned block of 256 rows (0 to 255, 256 to 511, ...) at most 4 rows name the same one
- agreement: int32 [16384], P('dp'), may hold values 0 or 1
- targets: int32 [16384], P('dp'), may hold values from 0 to 4999
- lengths: int32 [64], P('dp'), may hold values from 64 to 256
- student_hidden: bfloat16 [32768, 1024], P(('teach', 'dp')), may hold values from -6 to 6
- out_weight: bfloat16 [1024, 5000], replicated, may hold values from -2 to 2
- out_bias: float32 [5000], replicated, may hold values from -6 to 6
- gain: float32 [1024], replicated, may hold values from 0.5 to 1.5
Outputs:
- weight_grad: float32 [1024, 5000], P(('teach', 'dp'))
- gain_grad: float32 [1024], replicated
- bias_grad: float32 [5000], replicated
- loss: float32 [], replicated
Inputs may be any that keep to these rules, and one draw needn't show every extreme that they name: `routes`: within the 256 rows of one index of dp, each student device is named at most 4 times, and some device exactly 4 times.
All inputs are finite; a program needn't handle non-finite values. No bound on the sum of `agreement` on one device may be relied on, other than what follows from the above.
Results may differ from a plain program's by a relative error of at most 0.0031.
Values may be sent and summed in bfloat16 or wider, within the bound.
A program may use at most 128 MiB of HBM per device.

v0:
```python
import jax
import jax.numpy as jnp
from jax import lax
from jax.sharding import Mesh
from jax.sharding import PartitionSpec as P

LMAX = 256
DP = ("dp_0", "dp_1", "dp_2")
TEACH_DP = ("teach", "dp_0", "dp_1", "dp_2")
EPSILON = 1e-05


def over_axes(x, axes):
    for axis in axes:
        x = lax.psum(x, axis)
    return x


def route_slots(dest_device, devices):
    onehot = (dest_device[:, None] == jnp.arange(devices, dtype=jnp.int32)[None, :]).astype(
        jnp.float32
    )
    row_ids = jnp.arange(dest_device.shape[0], dtype=jnp.int32)
    earlier = (row_ids[None, :] < row_ids[:, None]).astype(jnp.float32)
    before = jnp.dot(
        earlier, onehot, preferred_element_type=jnp.float32, precision=lax.Precision.HIGHEST
    )
    return jnp.sum(before * onehot, axis=1).astype(jnp.int32)


def live_mask(lengths_block, row_total):
    row_ids = jnp.arange(row_total, dtype=jnp.int32)
    utterance = row_ids // LMAX
    frame_pos = row_ids % LMAX
    picks = utterance[:, None] == jnp.arange(lengths_block.shape[0], dtype=jnp.int32)[None, :]
    row_length = jnp.sum(jnp.where(picks, lengths_block[None, :], 0), axis=1)
    return (frame_pos < row_length).astype(jnp.float32)


def soft_targets(teacher_rows, agree_rows, target_rows, live_rows):
    probs_teacher = jax.nn.softmax(teacher_rows.astype(jnp.float32), axis=-1)
    onehot = (
        target_rows[:, None] == jnp.arange(probs_teacher.shape[1], dtype=jnp.int32)[None, :]
    ).astype(jnp.float32)
    weight = (0.5 * agree_rows.astype(jnp.float32))[:, None]
    return (live_rows[:, None] * (weight * probs_teacher + 0.5 * onehot)).astype(jnp.bfloat16)


def student_forward(hidden_rows, gain, out_weight, out_bias):
    states = hidden_rows.astype(jnp.float32)
    centre = jnp.mean(states, axis=1, keepdims=True)
    spread = jnp.mean(jnp.square(states - centre), axis=1, keepdims=True)
    normed = (states - centre) * lax.rsqrt(spread + EPSILON)
    scaled = (normed * gain[None, :]).astype(jnp.bfloat16)
    logits = jnp.dot(scaled, out_weight, preferred_element_type=jnp.float32) + out_bias[None, :]
    return (normed, scaled, jax.nn.log_softmax(logits, axis=-1))


def combined_grads(first_soft, second_soft, log_probs):
    first_float = first_soft.astype(jnp.float32)
    second_float = second_soft.astype(jnp.float32)
    row_mass = jnp.sum(first_float + second_float, axis=1, keepdims=True)
    return (row_mass * jnp.exp(log_probs) - first_float - second_float).astype(jnp.bfloat16)


def body(
    teacher_logits, routes, agreement, targets, lengths, student_hidden, out_weight, out_bias, gain
):
    teach_count = lax.axis_size("teach")
    data_count = lax.axis_size(DP)
    devices = teach_count * data_count
    rows_here = teacher_logits.shape[1]
    most_slots = 2 * rows_here // devices
    vocab = teacher_logits.shape[2]
    width = student_hidden.shape[1]
    dest_device = routes[:, 0]
    slot_index = route_slots(dest_device, devices)
    live_rows = live_mask(lengths, rows_here)
    soft_rows = soft_targets(teacher_logits[0], agreement, targets, live_rows)
    half = rows_here // 2
    first_here = lax.axis_index("teach") * half
    count_term = jnp.sum(lax.dynamic_slice_in_dim(live_rows, first_here, half, 0))
    stacked = soft_rows.reshape(2, half, vocab)
    both_soft = lax.all_to_all(stacked, "teach", split_axis=0, concat_axis=0, tiled=True)
    dest_half = lax.dynamic_slice_in_dim(dest_device, first_here, half, 0)
    slot_half = lax.dynamic_slice_in_dim(slot_index, first_here, half, 0)
    replicated = jnp.broadcast_to(
        student_hidden.reshape(1, data_count, most_slots, width),
        (teach_count, data_count, most_slots, width),
    ).reshape(devices, most_slots, width)
    arrived = lax.all_to_all(replicated, TEACH_DP, split_axis=0, concat_axis=0, tiled=True)
    hidden_rows = arrived[dest_half, slot_half]
    norm_rows, state_rows, log_probs = student_forward(hidden_rows, gain, out_weight, out_bias)
    grad_rows = combined_grads(both_soft[0], both_soft[1], log_probs)
    loss_term = -jnp.sum(
        (both_soft[0].astype(jnp.float32) + both_soft[1].astype(jnp.float32)) * log_probs
    )
    back_rows = lax.dot_general(
        grad_rows, out_weight, (((1,), (1,)), ((), ())), preferred_element_type=jnp.float32
    )
    gain_grad = jnp.sum(back_rows * norm_rows, axis=0)
    bias_grad = jnp.sum(grad_rows.astype(jnp.float32), axis=0)
    weight_grad = lax.psum_scatter(
        lax.dot_general(
            state_rows, grad_rows, (((0,), (0,)), ((), ())), preferred_element_type=jnp.float32
        ),
        TEACH_DP,
        scatter_dimension=0,
        tiled=True,
    )
    gain_sum, bias_sum, loss_sum, total_frames = (
        over_axes(gain_grad, TEACH_DP),
        over_axes(bias_grad, TEACH_DP),
        over_axes(loss_term, TEACH_DP),
        over_axes(count_term, TEACH_DP),
    )
    inverse = 1.0 / total_frames
    return (weight_grad * inverse, gain_sum * inverse, bias_sum * inverse, loss_sum * inverse)


def solution(mesh):
    finer = Mesh(
        mesh.devices.reshape(mesh.shape["teach"], 4, 4, 4), ("teach", "dp_0", "dp_1", "dp_2")
    )
    in_specs = (
        P("teach", DP, None),
        P(DP, None),
        P(DP),
        P(DP),
        P(DP),
        P(TEACH_DP, None),
        P(),
        P(),
        P(),
    )
    out_specs = (P(TEACH_DP, None), P(), P(), P())
    return jax.shard_map(body, mesh=finer, in_specs=in_specs, out_specs=out_specs, check_vma=False)
```

profile of v0, /device:TPU:1, one launch (start us, length us, event | category | flops | bytes accessed | tf_op | source)
XLA Modules:
  0.0 780.8 jit_solution(15204521626412033606)
XLA Ops:
  7.2 1.4 broadcast_in_dim.22
  8.6 1.2 broadcast_in_dim.23
  9.8 11.9 %all-to-all-start = ((bf16[128,4,1024]{2,1,0:T(4,128)(2,1)}), bf16[128,4,1024]{2,1,0:T(4,128)(2,1)}, u32[]{:S(2)}, u32[]{:S(2)}) async-start(bf16[128,4,1024]{2,1,0:T(4,128)(2,1)} %bitcast.51), calls=%async_computation | async-start | bytes 2097152 | tf_op jit(solution)/shard_map/all_to_all | solution.py:91
  22.4 4.0 copy.13
  26.4 0.7 reduce_max.28
  27.1 0.0 copy-done.7
  27.1 0.2 fusion.5
  27.4 0.9 fusion.1
  28.3 5.9 copy.14
  34.2 0.1 fusion.18
  34.3 5.7 multiply_convert_fusion
  40.0 6.1 all-to-all-start.1
  46.1 2.3 gather_fusion
  48.4 0.1 convert_reduce_fusion.1
  48.5 0.2 fusion.10
  48.8 6.3 fusion.23
  55.1 0.7 exponential_reduce_fusion
  55.8 3.0 multiply_reduce_fusion
  58.8 2.7 convert_reduce_fusion
  61.5 1.0 copy-done.1
  62.5 8.7 %fusion.19 = f32[1024,5000]{1,0:T(8,128)} fusion(bf16[128,5000]{0,1:T(8,128)(2,1)S(1)} %get-tuple-element.23, bf16[128,1024]{1,0:T(8,128)(2,1)S(1)} %gather_fusion, f32[1024]{0:T(1024)S(1)} %copy-done.3, f32[128]{0:T(128)S(1)} %add_rsqrt_fusion, f32[128]{0:T(128)S(1)} %broadcast_multiply_fusion.3), kind=kOutput, calls=%fused_computation.58 | convolution fusion | flops 1311375360 | bytes 22027264 | tf_op jit(solution)/shard_map/dot_general | solution.py:104
  71.2 0.0 reduce-scatter.2.cloned.1.call-update
  71.2 0.7 dynamic-slice_reduce_fusion
  72.6 5.6 fusion.4
  78.2 4.5 all-reduce.3
  82.8 14.6 %all-reduce.2 = (f32[]{:T(128)}, f32[1024]{0:T(1024)S(1)}, f32[5000]{0:T(1024)S(1)}, f32[]{:T(128)}) all-reduce(f32[]{:T(128)} %get-tuple-element.18, f32[1024]{0:T(1024)S(1)} %get-tuple-element.19, f32[5000]{0:T(1024)S(1)} %get-tuple-element.20, f32[]{:T(128)} %get-tuple-element.21), channel_id=1, replica_groups=mesh['teach'=2,'dp_0'=4,'dp_1'=4,'dp_2'=4] {'dp_0'}, use_global_device_ids=true, to_apply=%region_11.12 | all-reduce | flops 6026 | bytes 48208 | tf_op jit(solution)/shard_map/psum | solution.py:15
  97.3 16.6 %all-reduce.1 = (f32[]{:T(128)}, f32[1024]{0:T(1024)S(1)}, f32[5000]{0:T(1024)S(1)}, f32[]{:T(128)}) all-reduce(f32[]{:T(128)} %get-tuple-element.14, f32[1024]{0:T(1024)S(1)} %get-tuple-element.15, f32[5000]{0:T(1024)S(1)} %get-tuple-element.16, f32[]{:T(128)} %get-tuple-element.17), channel_id=1, replica_groups=mesh['teach'=2,'dp_0'=4,'dp_1'=4,'dp_2'=4] {'dp_1'}, use_global_device_ids=true, to_apply=%region_12.13 | all-reduce | flops 6026 | bytes 48208 | tf_op jit(solution)/shard_map/psum | solution.py:15
  114.0 15.5 %all-reduce = (f32[]{:T(128)}, f32[1024]{0:T(1024)S(1)}, f32[5000]{0:T(1024)S(1)}, f32[]{:T(128)}) all-reduce(f32[]{:T(128)} %get-tuple-element.10, f32[1024]{0:T(1024)S(1)} %get-tuple-element.11, f32[5000]{0:T(1024)S(1)} %get-tuple-element.12, f32[]{:T(128)} %get-tuple-element.13), channel_id=1, replica_groups=mesh['teach'=2,'dp_0'=4,'dp_1'=4,'dp_2'=4] {'dp_2'}, use_global_device_ids=true, to_apply=%region_13.14 | all-reduce | flops 6026 | bytes 48208 | tf_op jit(solution)/shard_map/psum | solution.py:15
  130.8 0.6 broadcast_multiply_fusion.2
  131.4 0.6 broadcast_multiply_fusion.1
  132.0 639.2 %reduce-scatter.2.cloned.1.call-done = f32[8,5000]{1,0:T(8,128)} async-done(((f32[1024,5000]{1,0:T(8,128)}), f32[8,5000]{1,0:T(8,128)}) %reduce-scatter.2.cloned.1.call-update) | async-done | bytes 160016 | tf_op jit(solution)/shard_map/reduce_scatter | solution.py:103
  771.2 1.6 broadcast_multiply_fusion
  (25 shorter events, 0.1 us)
Async XLA Ops:
  7.2 15.3 %copy-start = (bf16[1,256,5000]{1,2,0:T(8,128)(2,1)S(1)}, bf16[1,256,5000]{1,2,0:T(8,128)(2,1)}, u32[]{:S(2)}) copy-start(bf16[1,256,5000]{1,2,0:T(8,128)(2,1)} %param.9) | copy-start | bytes 7680004
  9.8 30.2 %all-to-all-start = ((bf16[128,4,1024]{2,1,0:T(4,128)(2,1)}), bf16[128,4,1024]{2,1,0:T(4,128)(2,1)}, u32[]{:S(2)}, u32[]{:S(2)}) async-start(bf16[128,4,1024]{2,1,0:T(4,128)(2,1)} %bitcast.51), calls=%async_computation | async-start | bytes 2097152 | tf_op jit(solution)/shard_map/all_to_all | solution.py:91
  26.4 0.7 copy-start.6
  26.4 0.7 copy-start.7
  28.3 6.0 copy-start.5
  40.0 15.8 %all-to-all-start.1 = ((bf16[2,128,5000]{1,2,0:T(8,128)(2,1)}), bf16[2,128,5000]{1,2,0:T(8,128)(2,1)}, u32[]{:S(2)}, u32[]{:S(2)}) async-start(bf16[2,128,5000]{1,2,0:T(8,128)(2,1)} %multiply_convert_fusion), calls=%async_computation.1 | async-start | bytes 5120000 | tf_op jit(solution)/shard_map/all_to_all | solution.py:84
  46.1 2.7 copy-start.3
  46.1 2.7 copy-start.4
  46.1 725.1 %reduce-scatter.2.cloned.1.call-start = ((), (), s32[]{:S(2)}) async-start(), calls=%async_computation.3 | async-start | bytes 21135360 | tf_op jit(solution)/shard_map/reduce_scatter | solution.py:103
  61.5 1.0 copy-start.1
  71.2 1.4 copy-start.2
Sparse Core Ops, SparseCore 0:
  71.3 699.7 reduce-scatter.1
where the time goes:
time: 781 us
  waiting for transfers between devices  639 us (82%)
  blocking collectives  51.3 us (7%)
  matrix products  20.9 us (3%)
  starting transfers between devices  18.1 us (2%)
  between operations  17.9 us (2%)
  other arithmetic  17.5 us (2%)
  local copies, waits for them, and re-layouts  15.9 us (2%)
    reduce_scatter x1, waiting for transfers between devices, body(): lax.psum_scatter(lax.dot_general(state_rows, grad_rows, (((0,), (0,)), ((...  639 us
    psum x4, blocking collectives, over_axes(): x = lax.psum(x, axis)  51.3 us
  transfers between devices with their start and end apart: 3, of which 1 were waited for; matrix products, arithmetic and copies ran while one was open for 4% of the time, Pallas kernels for 0%

commit v1 on v0

--- a/solution.py
+++ b/solution.py
@@ -12,7 +12,7 @@
 
 def over_axes(x, axes):
     for axis in axes:
-        x = lax.psum(x, axis)
+        x = jnp.sum(lax.all_gather(x, axis), axis=0)
     return x
 
 

time: 781 us -> 885 us (1.13)
  waiting for transfers between devices: 639 us -> 696 us
  local copies, waits for them, and re-layouts: 15.9 us -> 34.5 us
  blocking collectives: 51.3 us -> 68.3 us
    unnamed x1 -> x7, waiting for transfers between devices: 0.02 us -> 78.8 us
    psum x4 -> x0, blocking collectives: 51.3 us -> none  [over_axes(): x = lax.psum(x, axis)]
    all_gather x0 -> x4, blocking collectives: none -> 38.9 us  [over_axes(): x = jnp.sum(lax.all_gather(x, axis), axis=0)]
    unnamed x0 -> x4, blocking collectives: none -> 29.4 us
    reduce_scatter x1, waiting for transfers between devices: 639 us -> 617 us  [body(): lax.psum_scatter(lax.dot_general(state_rows, grad_rows, (((0,), (0,)), ((...]
    unnamed x16 -> x56, local copies, waits for them, and re-layouts: 1.06 us -> 16.6 us
  transfers between devices with their start and end apart: 3 -> 6, of which waited for: 1 -> 3; matrix products, arithmetic and copies ran while one was open for 4% -> 7% of each run, Pallas kernels for 0% -> 0%
where the time goes in v1:
time: 885 us; the launch traced here: 884 us
  waiting for transfers between devices  696 us (79%)
  blocking collectives  68.3 us (8%)
  local copies, waits for them, and re-layouts  34.5 us (4%)
  other arithmetic  23.6 us (3%)
  matrix products  22.2 us (3%)
  between operations  21.9 us (2%)
  starting transfers between devices  18.2 us (2%)
    reduce_scatter x1, waiting for transfers between devices, body(): lax.psum_scatter(lax.dot_general(state_rows, grad_rows, (((0,), (0,)), ((...  617 us
    unnamed x7, waiting for transfers between devices  78.8 us
    all_gather x4, blocking collectives, over_axes(): x = jnp.sum(lax.all_gather(x, axis), axis=0)  38.9 us
    unnamed x4, blocking collectives  29.4 us
  transfers between devices with their start and end apart: 6, of which 3 were waited for; matrix products, arithmetic and copies ran while one was open for 7% of the time, Pallas kernels for 0%

profile of v1, /device:TPU:1, one launch (start us, length us, event | category | flops | bytes accessed | tf_op | source)
XLA Modules:
  0.0 884.3 jit_solution(9101328733941864550)
XLA Ops:
  8.0 1.4 broadcast_in_dim.22
  9.4 1.2 broadcast_in_dim.23
  10.7 11.9 %all-to-all-start = ((bf16[128,4,1024]{2,1,0:T(4,128)(2,1)}), bf16[128,4,1024]{2,1,0:T(4,128)(2,1)}, u32[]{:S(2)}, u32[]{:S(2)}) async-start(bf16[128,4,1024]{2,1,0:T(4,128)(2,1)} %bitcast.67), calls=%async_computation | async-start | bytes 2097152 | tf_op jit(solution)/shard_map/all_to_all | solution.py:91
  24.5 4.0 copy.17
  31.1 5.9 copy.18
  37.7 1.4 dynamic-update-slice
  39.1 5.7 multiply_convert_fusion
  44.8 6.1 all-to-all-start.1
  50.9 2.3 gather_fusion
  53.6 6.4 fusion.23
  60.6 3.0 multiply_reduce_fusion
  65.2 3.7 convert_reduce_fusion
  69.8 3.5 all-reduce.15
  75.9 37.9 %all-reduce.20.cloned.1.call-done = f32[20000]{0:T(1024)} async-done(((f32[20000]{0:T(1024)}), f32[20000]{0:T(1024)}) %all-reduce.20.cloned.1.call-update) | async-done | bytes 80016
  117.2 40.9 %all-reduce.22.cloned.1.call-done = f32[20000]{0:T(1024)} async-done(((f32[20000]{0:T(1024)}), f32[20000]{0:T(1024)}) %all-reduce.22.cloned.1.call-update) | async-done | bytes 80016
  160.4 9.9 %fusion.19 = f32[1024,5000]{1,0:T(8,128)} fusion(bf16[128,5000]{0,1:T(8,128)(2,1)} %get-tuple-element.16, bf16[128,1024]{1,0:T(8,128)(2,1)S(1)} %gather_fusion, f32[1024]{0:T(1024)S(1)} %copy-done.5, f32[128]{0:T(128)S(1)} %add_rsqrt_fusion, f32[128]{0:T(128)S(1)} %broadcast_multiply_fusion.3), kind=kOutput, calls=%fused_computation.58 | convolution fusion | flops 1311375360 | bytes 22027264 | tf_op jit(solution)/shard_map/dot_general | solution.py:104
  171.5 1.4 dynamic-update-slice.9
  172.9 1.4 dynamic-update-slice.1
  174.3 8.7 all-reduce.14
  184.2 1.4 dynamic-update-slice.10
  185.6 1.4 dynamic-update-slice.2
  187.0 8.2 all-reduce.13
  196.4 1.4 dynamic-update-slice.11
  197.8 1.4 dynamic-update-slice.3
  199.2 9.0 %all-reduce.12 = (f32[4]{0:T(128)S(1)}, f32[4]{0:T(128)S(1)}) all-reduce(f32[4]{0:T(128)S(1)} %dynamic-update-slice.3, f32[4]{0:T(128)S(1)} %dynamic-update-slice.11), channel_id=1, replica_groups=mesh['teach'=2,'dp_0'=4,'dp_1'=4,'dp_2'=4] {'dp_2'}, use_global_device_ids=true, to_apply=%add.3 | all-reduce | flops 8 | bytes 64
  208.2 5.6 fusion.4
  213.8 9.1 %all-gather = f32[2048]{0:T(1024)S(1)} all-gather(f32[1024]{0:T(1024)S(1)} %fusion.4), channel_id=2, replica_groups=mesh['teach'=2,'dp_0'=4,'dp_1'=4,'dp_2'=4] {'teach'}, dimensions={0}, use_global_device_ids=true | all-gather | bytes 12288 | tf_op jit(solution)/shard_map/all_gather | solution.py:15
  222.9 9.8 %all-gather.1 = f32[4096]{0:T(1024)S(1)} all-gather(f32[1024]{0:T(1024)S(1)} %reduce_sum.251), channel_id=3, replica_groups=mesh['teach'=2,'dp_0'=4,'dp_1'=4,'dp_2'=4] {'dp_0'}, dimensions={0}, use_global_device_ids=true | all-gather | bytes 20480 | tf_op jit(solution)/shard_map/all_gather | solution.py:15
  232.7 10.0 %all-gather.2 = f32[4096]{0:T(1024)S(1)} all-gather(f32[1024]{0:T(1024)S(1)} %reduce_sum.252), channel_id=4, replica_groups=mesh['teach'=2,'dp_0'=4,'dp_1'=4,'dp_2'=4] {'dp_1'}, dimensions={0}, use_global_device_ids=true | all-gather | bytes 20480 | tf_op jit(solution)/shard_map/all_gather | solution.py:15
  242.7 10.1 %all-gather.3 = f32[4096]{0:T(1024)S(1)} all-gather(f32[1024]{0:T(1024)S(1)} %reduce_sum.253), channel_id=5, replica_groups=mesh['teach'=2,'dp_0'=4,'dp_1'=4,'dp_2'=4] {'dp_2'}, dimensions={0}, use_global_device_ids=true | all-gather | bytes 20480 | tf_op jit(solution)/shard_map/all_gather | solution.py:15
  257.7 616.8 %reduce-scatter.2.cloned.1.call-done = f32[8,5000]{1,0:T(8,128)} async-done(((f32[1024,5000]{1,0:T(8,128)}), f32[8,5000]{1,0:T(8,128)}) %reduce-scatter.2.cloned.1.call-update) | async-done | bytes 160016 | tf_op jit(solution)/shard_map/reduce_scatter | solution.py:103
  874.4 1.6 broadcast_multiply_fusion
  (102 shorter events, 20.2 us)
Async XLA Ops:
  8.0 15.3 %copy-start.13 = (u32[128]{0:T(128)S(1)}, u32[128]{0:T(128)}, u32[]{:S(2)}) copy-start(u32[128]{0:T(128)} %constant.103) | copy-start | bytes 1540
  8.0 15.9 %copy-start.12 = (u32[128]{0:T(128)S(1)}, u32[128]{0:T(128)}, u32[]{:S(2)}) copy-start(u32[128]{0:T(128)} %constant.98) | copy-start | bytes 1540
  8.0 16.5 %copy-start = (bf16[1,256,5000]{1,2,0:T(8,128)(2,1)S(1)}, bf16[1,256,5000]{1,2,0:T(8,128)(2,1)}, u32[]{:S(2)}) copy-start(bf16[1,256,5000]{1,2,0:T(8,128)(2,1)} %param.9) | copy-start | bytes 7680004
  10.7 34.1 %all-to-all-start = ((bf16[128,4,1024]{2,1,0:T(4,128)(2,1)}), bf16[128,4,1024]{2,1,0:T(4,128)(2,1)}, u32[]{:S(2)}, u32[]{:S(2)}) async-start(bf16[128,4,1024]{2,1,0:T(4,128)(2,1)} %bitcast.67), calls=%async_computation | async-start | bytes 2097152 | tf_op jit(solution)/shard_map/all_to_all | solution.py:91
  28.5 0.7 copy-start.8
  28.5 0.7 copy-start.9
  31.1 8.0 copy-start.7
  44.8 15.9 %all-to-all-start.1 = ((bf16[2,128,5000]{1,2,0:T(8,128)(2,1)}), bf16[2,128,5000]{1,2,0:T(8,128)(2,1)}, u32[]{:S(2)}, u32[]{:S(2)}) async-start(bf16[2,128,5000]{1,2,0:T(8,128)(2,1)} %multiply_convert_fusion), calls=%async_computation.1 | async-start | bytes 5120000 | tf_op jit(solution)/shard_map/all_to_all | solution.py:84
  50.9 2.7 copy-start.5
  50.9 2.7 copy-start.6
  50.9 62.9 %all-reduce.20.cloned.1.call-start = ((), (), s32[]{:S(2)}) async-start(), calls=%async_computation.4 | async-start | bytes 163840
  65.1 9.5 %copy-start.11 = (u32[128]{0:T(128)S(1)}, u32[128]{0:T(128)}, u32[]{:S(2)}) copy-start(u32[128]{0:T(128)} %constant.108) | copy-start | bytes 1540
  65.2 50.9 %copy-start.10 = (u32[128]{0:T(128)S(1)}, u32[128]{0:T(128)}, u32[]{:S(2)}) copy-start(u32[128]{0:T(128)} %constant.113) | copy-start | bytes 1540
  73.9 0.6 copy-start.2
  74.6 83.5 %all-reduce.22.cloned.1.call-start = ((), (), s32[]{:S(2)}) async-start(), calls=%async_computation.5 | async-start | bytes 163840
  115.3 0.6 copy-start.3
  116.0 140.0 %all-reduce.24.cloned.1.call-start = ((), (), s32[]{:S(2)}) async-start(), calls=%async_computation.6 | async-start | bytes 163840
  159.7 0.6 copy-start.4
  160.3 714.1 %reduce-scatter.2.cloned.1.call-start = ((), (), s32[]{:S(2)}) async-start(), calls=%async_computation.3 | async-start | bytes 21135360 | tf_op jit(solution)/shard_map/reduce_scatter | solution.py:103
  170.3 37.8 %copy-start.1 = (bf16[128,5000]{0,1:T(8,128)(2,1)S(1)}, bf16[128,5000]{0,1:T(8,128)(2,1)}, u32[]{:S(2)}) copy-start(bf16[128,5000]{0,1:T(8,128)(2,1)} %get-tuple-element.16) | copy-start | bytes 3840004
Sparse Core Ops, SparseCore 0:
  74.7 39.0 all-reduce.19
  116.7 41.4 all-reduce.21
  161.0 41.9 all-reduce.23
Sparse Core Ops, SparseCore 1:
  170.4 703.9 reduce-scatter.1
